TPU v7x, 32 devices: a whole 2x2x4 slice. The times are simulated.
32 devices in a mesh: dp: 4 (over z), ctx: 4 (over y, core), tp: 2 (over x).
Axes of the slice: x: 2, y: 2, z: 4, core: 2. Of those that a mesh axis runs over, the one named last changes fastest.
Arguments:
- hidden: bfloat16 [4, 512, 4096], P('dp', 'ctx'), may hold values from -6 to 6
- query_heads: bfloat16 [4, 512, 4096], P('dp', 'ctx', 'tp'), may hold values from -6 to 6
- key_heads: bfloat16 [4, 512, 512], P('dp', 'ctx', 'tp'), may hold values from -6 to 6
- value_heads: bfloat16 [4, 512, 512], P('dp', 'ctx', 'tp'), may hold values from -6 to 6
- attention_out: bfloat16 [4, 512, 4096], P('dp', 'ctx', 'tp'), may hold values from -3 to 3
- output_grad: bfloat16 [4, 512, 4096], P('dp', 'ctx', 'tp'), may hold values from -3 to 3
- log_norm: float32 [4, 32, 512], P('dp', 'tp', 'ctx'), may hold values from -40 to 40, as said below
- block_order: int32 [8], replicated, may hold values from 0 to 7, as said below
- value_weight: bfloat16 [4096, 512], P(None, 'tp'), may hold values from -0.25 to 0.25
Outputs:
- query_grad: bfloat16 [4, 512, 4096], P('dp', 'ctx', 'tp')
- key_grad: bfloat16 [4, 512, 512], P('dp', 'ctx', 'tp')
- value_grad: bfloat16 [4, 512, 512], P('dp', 'ctx', 'tp')
- hidden_grad: bfloat16 [4, 512, 4096], P('dp', 'ctx', 'tp')
- weight_grad: float32 [4096, 512], P('ctx', 'tp')
Inputs may be any that keep to these rules, and one draw needn't show every extreme that they name: `block_order`: each of 0 to 7 once. log_norm is the log of the sum of exp(scores) over the keys visible to that row, so the probabilities of each row and head sum to one.
All inputs are finite; a program needn't handle non-finite values.
Results may differ from a plain program's by a relative error of at most 0.025.
Values may be sent and summed in bfloat16 or wider, within the bound.
A program may use at most 64 MiB of HBM per device.

v0:
```python
import math

import jax
import jax.numpy as jnp
from jax import lax
from jax.sharding import PartitionSpec as P

HD = 128
HQ = 32
KVH = 4


def block_positions(row_ids, block_order, block_len):
    labels = jnp.arange(block_order.shape[0], dtype=jnp.int32)
    picked = jnp.where((row_ids // block_len)[:, None] == labels[None, :], block_order[None, :], 0)
    return jnp.sum(picked, axis=1) * block_len + row_ids % block_len


def shards(
    hidden,
    query_heads,
    key_heads,
    value_heads,
    attention_out,
    output_grad,
    log_norm,
    block_order,
    value_weight,
):
    tokens = query_heads.shape[1]
    local_heads = key_heads.shape[2] // HD
    members = HQ // KVH
    block_len = tokens // 2
    cycle_size = lax.axis_size("ctx")
    cycle_rank = lax.axis_index("ctx")
    score_scale = HD ** (-0.5)
    local_rows = cycle_rank * tokens + jnp.arange(tokens, dtype=jnp.int32)
    query_pos = block_positions(local_rows, block_order, block_len)
    query_rows = query_heads[0].reshape(tokens, local_heads, members, HD)
    out_rows = attention_out[0].reshape(tokens, local_heads, members, HD)
    grad_rows = output_grad[0].reshape(tokens, local_heads, members, HD)
    row_delta = jnp.einsum(
        "tgjd,tgjd->gjt", grad_rows, out_rows, preferred_element_type=jnp.float32
    )
    norm_rows = log_norm[0].reshape(local_heads, members, tokens)

    def attend(running, key_block, value_block, block_first):
        key_count = key_block.shape[0]
        key_ids = block_first + jnp.arange(key_count, dtype=jnp.int32)
        key_pos = block_positions(key_ids, block_order, block_len)
        visible = key_pos[None, :] <= query_pos[:, None]
        acc_query, acc_key, acc_value = running
        scores = (
            jnp.einsum("tgjd,kgd->gjtk", query_rows, key_block, preferred_element_type=jnp.float32)
            * score_scale
        )
        shifted = jnp.where(visible[None, None], scores - norm_rows[:, :, :, None], -jnp.inf)
        probability = jnp.exp(shifted)
        weights = probability.astype(jnp.bfloat16)
        fresh_value = jnp.einsum(
            "gjtk,tgjd->kgd", weights, grad_rows, preferred_element_type=jnp.float32
        )
        through = jnp.einsum(
            "tgjd,kgd->gjtk", grad_rows, value_block, preferred_element_type=jnp.float32
        )
        slopes = (probability * (through - row_delta[:, :, :, None])).astype(jnp.bfloat16)
        acc_query = acc_query + jnp.einsum(
            "gjtk,kgd->tgjd", slopes, key_block, preferred_element_type=jnp.float32
        )
        fresh_key = jnp.einsum(
            "gjtk,tgjd->kgd", slopes, query_rows, preferred_element_type=jnp.float32
        )
        acc_key = lax.dynamic_update_slice_in_dim(
            acc_key,
            lax.dynamic_slice_in_dim(acc_key, block_first, key_count, 0) + fresh_key,
            block_first,
            0,
        )
        acc_value = lax.dynamic_update_slice_in_dim(
            acc_value,
            lax.dynamic_slice_in_dim(acc_value, block_first, key_count, 0) + fresh_value,
            block_first,
            0,
        )
        return (acc_query, acc_key, acc_value)

    def accumulate(running, pieces, first_row):
        key_piece, value_piece = pieces
        key_count = key_piece.shape[0]
        sub_width = math.gcd(key_count, 512)
        sub_turns = key_count // sub_width
        if sub_turns == 1:
            return attend(running, key_piece, value_piece, first_row)

        def advance(step_index, inner_state):
            offset = step_index * sub_width
            return attend(
                inner_state,
                lax.dynamic_slice_in_dim(key_piece, offset, sub_width, 0),
                lax.dynamic_slice_in_dim(value_piece, offset, sub_width, 0),
                first_row + offset,
            )

        return lax.fori_loop(0, sub_turns, advance, running)

    zeros_query = jnp.zeros((tokens, local_heads, members, HD), jnp.float32)
    zeros_pair = jnp.zeros((cycle_size * tokens, local_heads, HD), jnp.float32)
    key_local = key_heads[0].reshape(tokens, local_heads, HD)
    value_local = value_heads[0].reshape(tokens, local_heads, HD)
    acc_query, part_key, part_value = accumulate(
        (zeros_query, zeros_pair, zeros_pair),
        (
            lax.all_gather(key_local, "ctx", axis=0, tiled=True),
            lax.all_gather(value_local, "ctx", axis=0, tiled=True),
        ),
        jnp.int32(0),
    )
    own_key, own_value = (
        lax.psum_scatter(
            part_key.astype(jnp.bfloat16), "ctx", scatter_dimension=0, tiled=True
        ).astype(jnp.float32),
        lax.psum_scatter(
            part_value.astype(jnp.bfloat16), "ctx", scatter_dimension=0, tiled=True
        ).astype(jnp.float32),
    )
    query_grad = (
        (acc_query * score_scale)
        .astype(jnp.bfloat16)
        .reshape(1, tokens, local_heads * members * HD)
    )
    key_grad = (own_key * score_scale).astype(jnp.bfloat16).reshape(1, tokens, local_heads * HD)
    value_grad = own_value.astype(jnp.bfloat16).reshape(1, tokens, local_heads * HD)
    value_rows = value_grad[0]
    inputs = hidden[0]
    partial_term = jnp.einsum("td,te->de", inputs, value_rows, preferred_element_type=jnp.float32)
    row_share = lax.psum_scatter(
        lax.optimization_barrier(partial_term.astype(jnp.bfloat16))
        .astype(jnp.float32)
        .astype(jnp.bfloat16),
        "ctx",
        scatter_dimension=0,
        tiled=True,
    )
    summed_rows = lax.psum(row_share, "dp").astype(jnp.float32)
    token_norm = (lax.axis_size("dp") * cycle_size * tokens) ** (-0.5)
    weight_grad = summed_rows * token_norm
    partial_value = jnp.einsum(
        "te,de->td", value_rows, value_weight, preferred_element_type=jnp.float32
    )
    summed = lax.psum_scatter(
        partial_value.astype(jnp.bfloat16), "tp", scatter_dimension=1, tiled=True
    ).astype(jnp.float32)
    hidden_grad = summed.astype(jnp.bfloat16).reshape(1, tokens, summed.shape[1])
    return (query_grad, key_grad, value_grad, hidden_grad, weight_grad)


def solution(mesh):
    placed = (
        P("dp", "ctx", None),
        P("dp", "ctx", "tp"),
        P("dp", "ctx", "tp"),
        P("dp", "ctx", "tp"),
        P("dp", "ctx", "tp"),
        P("dp", "ctx", "tp"),
        P("dp", "tp", "ctx"),
        P(),
        P(None, "tp"),
    )
    return jax.shard_map(
        shards,
        mesh=mesh,
        in_specs=placed,
        out_specs=(
            P("dp", "ctx", "tp"),
            P("dp", "ctx", "tp"),
            P("dp", "ctx", "tp"),
            P("dp", "ctx", "tp"),
            P("ctx", "tp"),
        ),
        check_vma=False,
    )
```

profile of v0, /device:TPU:0, one launch (start us, length us, event | category | flops | bytes accessed | tf_op | source)
XLA Modules:
  0.0 174.6 jit_solution(1316045915267573734)
XLA Ops:
  7.3 0.9 select_reduce_fusion.1
  8.2 0.7 select_reduce_fusion
  8.9 0.9 copy.39
  10.0 7.3 %all_gather.6 = bf16[512,2,128]{2,0,1:T(8,128)(2,1)S(1)} all-gather(bf16[128,2,128]{2,0,1:T(8,128)(2,1)S(1)} %copy.40), channel_id=1, replica_groups=mesh['dp'=4,'ctx'=4,'tp'=2] {'ctx'}, dimensions={0}, use_global_device_ids=true | all-gather | bytes 327680 | tf_op jit(solution)/shard_map/all_gather | solution.py:113
  17.2 1.1 copy.72
  18.4 1.1 copy.73
  20.4 1.9 %copy-done.1 = f32[2,512,128,8]{2,1,3,0:T(8,128)} copy-done((f32[2,512,128,8]{2,1,3,0:T(8,128)}, f32[2,512,128,8]{2,1,3,0:T(8,128)S(1)}, u32[]{:S(2)}) %copy-start.1) | copy-done | bytes 4194328
  22.3 1.7 %fusion.17 = bf16[512,2,128]{2,0,1:T(8,128)(2,1)} fusion(f32[2,512,128,8]{2,1,3,0:T(8,128)S(1)} %fusion.26, f32[2,8,128]{2,1,0:T(8,128)S(1)} %bitcast.109, pred[128,512]{0,1:T(8,128)(4,1)S(1)} %broadcast_compare_fusion, bf16[128,2,8,128]{3,2,1,0:T(8,128)(2,1)S(1)} %bitcast.94), kind=kOutput, calls=%fused_computation.18 | convolution fusion | flops 272760832 | bytes 5054464 | tf_op jit(solution)/shard_map/gjtk,tgjd->kgd/dot_general | solution.py:60
  24.2 21.4 %reduce-scatter.7.cloned.1.call-done = bf16[128,2,128]{2,0,1:T(8,128)(2,1)} async-done(((bf16[512,2,128]{2,0,1:T(8,128)(2,1)}), bf16[128,2,128]{2,0,1:T(8,128)(2,1)}) %reduce-scatter.7.cloned.1.call-update) | async-done | bytes 65552 | tf_op jit(solution)/shard_map/reduce_scatter | solution.py:122
  45.6 0.9 copy.50
  46.6 3.3 %fusion = bf16[4096,256]{0,1:T(8,128)(2,1)} fusion(bf16[128,256]{0,1:T(8,128)(2,1)S(1)} %bitcast.99, bf16[1,128,4096]{2,1,0:T(8,128)(2,1)} %param.9), kind=kOutput, calls=%fused_computation.1 | convolution fusion | flops 269484032 | bytes 3211264 | tf_op jit(solution)/shard_map/td,te->de/dot_general | solution.py:135
  49.9 0.7 copy.42
  50.6 0.9 copy.43
  51.6 1.2 copy.74
  52.8 1.1 fusion.22
  53.9 1.0 copy.64
  54.8 5.8 %all_gather.7 = bf16[512,2,128]{2,0,1:T(8,128)(2,1)S(1)} all-gather(bf16[128,2,128]{2,0,1:T(8,128)(2,1)S(1)} %copy.43), channel_id=1, replica_groups=mesh['dp'=4,'ctx'=4,'tp'=2] {'ctx'}, dimensions={0}, use_global_device_ids=true | all-gather | bytes 327680 | tf_op jit(solution)/shard_map/all_gather | solution.py:114
  60.6 3.6 %fusion.2 = bf16[2,8,128,512]{2,3,1,0:T(8,128)(2,1)S(1)} fusion(f32[2,512,128,8]{2,1,3,0:T(8,128)} %copy-done.1, f32[2,8,128]{2,1,0:T(8,128)S(1)} %copy.64, f32[2,8,128]{2,1,0:T(8,128)S(1)} %bitcast.110, pred[128,512]{0,1:T(8,128)(4,1)} %copy-done.4, bf16[128,2,8,128]{3,2,1,0:T(8,128)(2,1)S(1)} %bitcast.96, bf16[512,2,128]{2,0,1:T(8,128)(2,1)S(1)} %all_gather.7), kind=kOutput, calls=%fused_computation.5 | convolution fusion | flops 274726912 | bytes 7159808 | tf_op jit(solution)/shard_map/tgjd,kgd->gjtk/dot_general | solution.py:63
  64.2 1.3 copy-done.2
  65.6 1.4 fusion.20
  67.1 14.1 %reduce-scatter.11.cloned.1.call-done = bf16[1024,256]{0,1:T(8,128)(2,1)} async-done(((bf16[4096,256]{0,1:T(8,128)(2,1)}), bf16[1024,256]{0,1:T(8,128)(2,1)}) %reduce-scatter.11.cloned.1.call-update) | async-done | bytes 524304 | tf_op jit(solution)/shard_map/reduce_scatter | solution.py:136
  81.3 1.8 %convolution_convert_fusion.1 = bf16[128,4096]{1,0:T(8,128)(2,1)} fusion(bf16[128,256]{0,1:T(8,128)(2,1)S(1)} %bitcast.100, bf16[4096,256]{1,0:T(8,128)(2,1)S(1)} %copy-done), kind=kOutput, calls=%fused_computation.2 | convolution fusion | flops 268959744 | bytes 3211264 | tf_op jit(solution)/shard_map/te,de->td/dot_general | solution.py:147
  83.1 2.1 %fusion.9 = bf16[2,8,128,128]{2,3,1,0:T(8,128)(2,1)S(1)} fusion(bf16[2,8,128,512]{2,3,1,0:T(8,128)(2,1)} %copy-done.2, bf16[512,2,128]{2,0,1:T(8,128)(2,1)S(1)} %all_gather.6), kind=kOutput, calls=%fused_computation.13 | convolution fusion | flops 268959744 | bytes 2883584 | tf_op jit(solution)/shard_map/gjtk,kgd->tgjd/dot_general | solution.py:67
  85.2 1.0 copy.52
  86.2 18.1 %reduce-scatter.5.cloned.1.call-done = bf16[128,2,128]{2,0,1:T(8,128)(2,1)} async-done(((bf16[512,2,128]{2,0,1:T(8,128)(2,1)}), bf16[128,2,128]{2,0,1:T(8,128)(2,1)}) %reduce-scatter.5.cloned.1.call-update) | async-done | bytes 65552 | tf_op jit(solution)/shard_map/reduce_scatter | solution.py:119
  104.3 0.9 multiply_convert_fusion
  105.3 0.7 copy.53
  106.0 0.7 copy.54
  106.8 38.4 %all-reduce.2.cloned.1.call-done = bf16[1024,256]{0,1:T(8,128)(2,1)} async-done(((bf16[1024,256]{0,1:T(8,128)(2,1)}), bf16[1024,256]{0,1:T(8,128)(2,1)}) %all-reduce.2.cloned.1.call-update) | async-done | bytes 524304 | tf_op jit(solution)/shard_map/psum | solution.py:144
  145.2 1.2 convert_multiply_fusion.1
  146.4 1.3 copy.55
  147.7 20.4 %reduce-scatter.9.cloned.1.call-done = bf16[128,2048]{1,0:T(8,128)(2,1)} async-done(((bf16[128,4096]{1,0:T(8,128)(2,1)}), bf16[128,2048]{1,0:T(8,128)(2,1)}) %reduce-scatter.9.cloned.1.call-update) | async-done | bytes 524304 | tf_op jit(solution)/shard_map/reduce_scatter | solution.py:150
  (28 shorter events, 1.4 us)
Async XLA Ops:
  7.2 74.1 %copy-start = (bf16[4096,256]{1,0:T(8,128)(2,1)S(1)}, bf16[4096,256]{1,0:T(8,128)(2,1)}, u32[]{:S(2)}) copy-start(bf16[4096,256]{1,0:T(8,128)(2,1)} %param.17) | copy-start | bytes 6291460
  7.2 15.2 %copy-start.5 = (f32[1,16,128]{2,1,0:T(8,128)S(1)}, f32[1,16,128]{2,1,0:T(8,128)}, u32[]{:S(2)}) copy-start(f32[1,16,128]{2,1,0:T(8,128)} %param.15) | copy-start | bytes 24580
  7.2 38.4 %reduce-scatter.7.cloned.1.call-start = ((), (), s32[]{:S(2)}) async-start(), calls=%async_computation.5 | async-start | bytes 327680 | tf_op jit(solution)/shard_map/reduce_scatter | solution.py:122
  19.7 4.4 %copy-start.4 = (pred[128,512]{0,1:T(8,128)(4,1)}, pred[128,512]{0,1:T(8,128)(4,1)S(1)}, u32[]{:S(2)}) copy-start(pred[128,512]{0,1:T(8,128)(4,1)S(1)} %broadcast_compare_fusion) | copy-start | bytes 196612
  20.4 1.9 %copy-start.1 = (f32[2,512,128,8]{2,1,3,0:T(8,128)}, f32[2,512,128,8]{2,1,3,0:T(8,128)S(1)}, u32[]{:S(2)}) copy-start(f32[2,512,128,8]{2,1,3,0:T(8,128)S(1)} %fusion.26) | copy-start | bytes 12582916
  24.1 25.8 %copy-start.3 = (bf16[1,128,256]{2,1,0:T(8,128)(2,1)S(1)}, bf16[1,128,256]{2,1,0:T(8,128)(2,1)}, u32[]{:S(2)}) copy-start(bf16[1,128,256]{2,1,0:T(8,128)(2,1)} %param.12) | copy-start | bytes 196612
  24.1 57.1 %reduce-scatter.11.cloned.1.call-start = ((), (), s32[]{:S(2)}) async-start(), calls=%async_computation.7 | async-start | bytes 2621440 | tf_op jit(solution)/shard_map/reduce_scatter | solution.py:136
  49.8 54.5 %reduce-scatter.5.cloned.1.call-start = ((), (), s32[]{:S(2)}) async-start(), calls=%async_computation.4 | async-start | bytes 327680 | tf_op jit(solution)/shard_map/reduce_scatter | solution.py:119
  64.2 1.4 copy-start.2
  67.0 78.2 %all-reduce.2.cloned.1.call-start = ((), (), s32[]{:S(2)}) async-start(), calls=%async_computation.8 | async-start | bytes 1048576 | tf_op jit(solution)/shard_map/psum | solution.py:144
  81.2 86.9 %reduce-scatter.9.cloned.1.call-start = ((), (), s32[]{:S(2)}) async-start(), calls=%async_computation.6 | async-start | bytes 1572864 | tf_op jit(solution)/shard_map/reduce_scatter | solution.py:150
Sparse Core Ops, SparseCore 0:
  24.2 21.3 reduce-scatter.6
  50.0 31.1 reduce-scatter.10
  84.2 20.0 reduce-scatter.4
  106.5 38.6 all-reduce.1
  147.9 20.1 reduce-scatter.8
where the time goes:
time: 175 us
  waiting for transfers between devices  113 us (65%)
  local copies, waits for them, and re-layouts  15.3 us (9%)
  matrix products  14.6 us (8%)
  between operations  14 us (8%)
  blocking collectives  13 us (7%)
  other arithmetic  4.91 us (3%)
    psum x1, waiting for transfers between devices, shards(): summed_rows = lax.psum(row_share, 'dp').astype(jnp.float32)  38.4 us
    reduce_scatter x1, waiting for transfers between devices, shards(): lax.psum_scatter(part_value.astype(jnp.bfloat16), 'ctx', scatter_dimensio...  21.4 us
    reduce_scatter x1, waiting for transfers between devices, shards(): lax.psum_scatter(partial_value.astype(jnp.bfloat16), 'tp', scatter_dimens...  20.4 us
    reduce_scatter x1, waiting for transfers between devices, shards(): lax.psum_scatter(part_key.astype(jnp.bfloat16), 'ctx', scatter_dimension=...  18.1 us
    reduce_scatter x1, waiting for transfers between devices, shards(): lax.psum_scatter(lax.optimization_barrier(partial_term.astype(jnp.bfloat1...  14.1 us
    unnamed x21, local copies, waits for them, and re-layouts  12.2 us
    all_gather x1, blocking collectives, shards(): lax.all_gather(key_local, 'ctx', axis=0, tiled=True)  7.25 us
    all_gather x1, blocking collectives, shards(): lax.all_gather(value_local, 'ctx', axis=0, tiled=True)  5.78 us
  transfers between devices with their start and end apart: 5, of which 5 were waited for; matrix products, arithmetic and copies ran while one was open for 11% of the time, Pallas kernels for 0%

commit v1 on v0

v1 whole, which is shorter than its diff:
```python
import functools

import jax
import jax.numpy as jnp
from jax import lax
from jax.experimental import pallas as pl
from jax.experimental.pallas import tpu as pltpu
from jax.sharding import PartitionSpec as P

HD = 128
HQ = 32
KVH = 4
F32 = jnp.float32
BF16 = jnp.bfloat16
MESH = pl.DeviceIdType.MESH


def dot(a, b, ca, cb):
    return lax.dot_general(a, b, (((ca,), (cb,)), ((), ())), preferred_element_type=F32)


def kernel(
    sizes,
    order_ref, k_ref, v_ref, norm_ref, hid_ref, q_ref, ao_ref, og_ref, vw_ref,
    dq_ref, dk_ref, dv_ref, dh_ref, dw_ref,
    qs, aos, ogs, kg, vg, hg, wg, ht, prob, acck, accv, bias,
    dvp, dvr, vown, vall, vtp, dkp, dkr, wp, zr, zown, zall,
    local_sem, send, recv,
):
    n, t, z, rows, groups, members, dn, dt, chunk, keyc = sizes
    me, mt, mz = lax.axis_index("ctx"), lax.axis_index("tp"), lax.axis_index("dp")
    keys = n * rows
    blk = rows // 2
    scale = HD ** (-0.5)
    width = 2 * rows
    pairs = members // 2

    loads = [
        pltpu.make_async_copy(q_ref, qs, local_sem.at[0]),
        pltpu.make_async_copy(og_ref, ogs, local_sem.at[1]),
        pltpu.make_async_copy(ao_ref, aos, local_sem.at[2]),
        pltpu.make_async_copy(
            hid_ref.at[0, :, pl.ds(pl.multiple_of(me * dn, 128), dn)], hg.at[me], local_sem.at[3]
        ),
        pltpu.make_async_copy(
            vw_ref.at[pl.ds(pl.multiple_of(mt * dt, 128), dt)], wg.at[mt], local_sem.at[4]
        ),
    ]
    for load in loads:
        load.start()

    peers = {"ctx": (me, n), "tp": (mt, t), "dp": (mz, z)}

    def others(axis):
        mine, count = peers[axis]
        return [lax.rem(mine + o, count) for o in range(1, count)]

    barrier = pltpu.get_barrier_semaphore()
    for axis in peers:
        for peer in others(axis):
            pl.semaphore_signal(barrier, inc=1, device_id={axis: peer}, device_id_type=MESH)
    pl.semaphore_wait(barrier, n - 1 + t - 1 + z - 1)

    used = [0]

    def fan(axis, source, target):
        made = []
        for o, peer in enumerate(others(axis)):
            copy = pltpu.make_async_remote_copy(
                src_ref=source(peer),
                dst_ref=target(o),
                send_sem=send.at[used[0]],
                recv_sem=recv.at[used[0]],
                device_id={axis: peer},
                device_id_type=MESH,
            )
            used[0] += 1
            copy.start()
            made.append(copy)
        return made

    my_rows = pl.ds(pl.multiple_of(me * rows, rows), rows)
    k_copies = fan("ctx", lambda p: k_ref.at[0], lambda o: kg.at[my_rows])
    v_copies = fan("ctx", lambda p: v_ref.at[0], lambda o: vg.at[my_rows])
    h_copies = fan(
        "ctx",
        lambda p: hid_ref.at[0, :, pl.ds(pl.multiple_of(p * dn, 128), dn)],
        lambda o: hg.at[me],
    )
    w_copies = fan(
        "tp", lambda p: vw_ref.at[pl.ds(pl.multiple_of(p * dt, 128), dt)], lambda o: wg.at[mt]
    )
    kg[my_rows] = k_ref[0]
    vg[my_rows] = v_ref[0]

    lane = lax.broadcasted_iota(jnp.int32, (blk, width), 1) % rows
    first = order_ref[2 * me] * blk
    second = order_ref[2 * me + 1] * blk
    query_pos = lane % blk + jnp.where(lane < blk, first, second)
    inside = lax.broadcasted_iota(jnp.int32, (blk, width), 0)
    for b in range(keys // blk):
        key_pos = inside + order_ref[b] * blk
        bias[b * blk : (b + 1) * blk] = jnp.where(key_pos <= query_pos, 0.0, -1e30).astype(F32)

    def two(ref, head):
        return jnp.concatenate(
            [ref[0, :, pl.ds(pl.multiple_of((head + j) * HD, HD), HD)] for j in range(2)], axis=0
        )

    def lanes(head):
        pieces = [norm_ref[0, pl.ds(head + j, 1), :] for j in range(2)]
        return jnp.concatenate(pieces, axis=1)

    loads[0].wait()
    loads[1].wait()
    for copy in k_copies:
        copy.wait_recv()

    def values(g):
        col = g * HD

        def pair(step, carry):
            head = g * members + step * 2
            q2, og2, norm = two(qs, head), two(ogs, head), lanes(head)

            def block(c, carry):
                at = pl.ds(pl.multiple_of(c * keyc, keyc), keyc)
                s = dot(kg[at, col : col + HD], q2, 1, 1) * scale
                p = jnp.exp(s + bias[at] - norm)
                prob[g * pairs + step, at] = p
                accv[g, at] += dot(p.astype(BF16), og2, 1, 0)
                return carry

            return lax.fori_loop(0, keys // keyc, block, carry)

        accv[g] = jnp.zeros((keys, HD), F32)
        lax.fori_loop(0, pairs, pair, 0)
        for s in range(n):
            dvp[g, s] = accv[g, s * rows : (s + 1) * rows].astype(BF16)
        return fan("ctx", lambda p: dvp.at[g, p], lambda o: dvr.at[g, o])

    def slopes(g):
        col = g * HD
        acck[g] = jnp.zeros((keys, HD), F32)

        def pair(step, carry):
            head = g * members + step * 2
            q2, og2 = two(qs, head), two(ogs, head)
            product = og2.astype(F32) * two(aos, head).astype(F32)
            delta = jnp.sum(product.T, axis=0, keepdims=True)

            def block(c, dq):
                at = pl.ds(pl.multiple_of(c * keyc, keyc), keyc)
                through = dot(vg[at, col : col + HD], og2, 1, 1)
                ds = (prob[g * pairs + step, at] * (through - delta)).astype(BF16)
                acck[g, at] += dot(ds, q2, 1, 0)
                return dq + dot(kg[at, col : col + HD].T, ds, 1, 0)

            dq = lax.fori_loop(0, keys // keyc, block, jnp.zeros((HD, width), F32))
            dq = (dq * scale).T.astype(BF16)
            for j in range(2):
                dq_ref[0, :, pl.ds(pl.multiple_of((head + j) * HD, HD), HD)] = dq[
                    j * rows : (j + 1) * rows
                ]
            return carry

        lax.fori_loop(0, pairs, pair, 0)
        for s in range(n):
            dkp[g, s] = acck[g, s * rows : (s + 1) * rows].astype(BF16)
        return fan("ctx", lambda p: dkp.at[g, p], lambda o: dkr.at[g, o])

    def reduced(copies, own, landed, g):
        for copy in copies:
            copy.wait_recv()
        total = own
        for o in range(n - 1):
            total = total + landed[g, o].astype(F32)
        return total

    def value_out(g, copies):
        col = g * HD
        total = reduced(copies, dvp[g, me].astype(F32), dvr, g).astype(BF16)
        dv_ref[0, :, col : col + HD] = total
        vown[g] = total
        made = fan("ctx", lambda p: vown.at[g], lambda o: vall.at[g, me])
        made_tp = fan("tp", lambda p: vown.at[g], lambda o: vtp.at[g, mt])
        vall[g, me] = total
        vtp[g, mt] = total
        return made, made_tp

    def weight_part(g, copies):
        for copy in copies:
            copy.wait_recv()
        size = min(dn, 256)

        def tile(i, carry):
            at = pl.ds(pl.multiple_of(i * size, size), size)
            rhs = vall[g].reshape(keys, HD)
            wp[g, at] = dot(ht[at], rhs, 1, 0).astype(BF16)
            return carry

        lax.fori_loop(0, dn // size, tile, 0)
        if z * chunk > dn:
            wp[g, dn:] = jnp.zeros((z * chunk - dn, HD), BF16)

        def piece(p):
            return wp.at[g, pl.ds(pl.multiple_of(p * chunk, 16), chunk)]

        return fan("dp", piece, lambda o: zr.at[g, o])

    def weight_sum(g, copies):
        for copy in copies:
            copy.wait_recv()
        mine = pl.ds(pl.multiple_of(mz * chunk, 16), chunk)
        total = wp[g, mine].astype(F32)
        for o in range(z - 1):
            total = total + zr[g, o].astype(F32)
        total = total.astype(BF16)
        zown[g] = total
        made = fan("dp", lambda p: zown.at[g], lambda o: zall.at[g, mine])
        zall[g, mine] = total
        return made

    dv_copies = [values(g) for g in range(groups)]
    gathers, shares, dk_copies, w_parts = [], [], [], []
    loads[2].wait()
    for copy in v_copies:
        copy.wait_recv()
    made, made_tp = value_out(0, dv_copies[0])
    gathers.append(made)
    shares.append(made_tp)
    dk_copies.append(slopes(0))
    for g in range(1, groups):
        made, made_tp = value_out(g, dv_copies[g])
        gathers.append(made)
        shares.append(made_tp)
    loads[3].wait()
    for copy in h_copies:
        copy.wait_recv()
    for s in range(n):
        ht[:, s * rows : (s + 1) * rows] = hg[s].T
    w_parts.append(weight_part(0, gathers[0]))
    for g in range(1, groups):
        w_parts.append(weight_part(g, gathers[g]))
    for g in range(1, groups):
        dk_copies.append(slopes(g))
    z_copies = [weight_sum(g, w_parts[g]) for g in range(groups)]

    loads[4].wait()
    for copy in w_copies:
        copy.wait_recv()
    for g in range(groups):
        for copy in shares[g]:
            copy.wait_recv()
    size = min(dt, 256)

    def out_tile(i, carry):
        at = pl.ds(pl.multiple_of(i * size, size), size)
        total = jnp.zeros((rows, size), F32)
        for p in range(t):
            lhs = jnp.concatenate([vtp[g, p] for g in range(groups)], axis=1)
            total = total + dot(lhs, wg[p, at], 1, 1)
        dh_ref[0, :, at] = total.astype(BF16)
        return carry

    lax.fori_loop(0, dt // size, out_tile, 0)

    for g in range(groups):
        col = g * HD
        total = reduced(dk_copies[g], dkp[g, me].astype(F32), dkr, g)
        dk_ref[0, :, col : col + HD] = (total * scale).astype(BF16)

    token_norm = (z * n * rows) ** (-0.5)
    for g in range(groups):
        for copy in z_copies[g]:
            copy.wait_recv()
        dw_ref[:, g * HD : (g + 1) * HD] = zall[g, :dn].astype(F32) * token_norm

    everything = k_copies + v_copies + h_copies + w_copies
    for group in dv_copies + gathers + shares + dk_copies + w_parts + z_copies:
        everything = everything + group
    for copy in everything:
        copy.wait_send()


def shards(
    hidden, query_heads, key_heads, value_heads, attention_out, output_grad,
    log_norm, block_order, value_weight,
):
    n, t, z = lax.axis_size("ctx"), lax.axis_size("tp"), lax.axis_size("dp")
    rows = query_heads.shape[1]
    depth = hidden.shape[2]
    cols = key_heads.shape[2]
    groups = cols // HD
    heads = query_heads.shape[2] // HD
    members = heads // groups
    dn, dt = depth // n, depth // t
    chunk = -(-dn // (16 * z)) * 16
    keys = n * rows
    keyc = min(keys, 512)
    sizes = (n, t, z, rows, groups, members, dn, dt, chunk, keyc)
    count = (n - 1) * (3 + 3 * groups) + (t - 1) * (1 + groups) + (z - 1) * 2 * groups
    vmem, anywhere = pl.BlockSpec(memory_space=pltpu.VMEM), pl.BlockSpec(memory_space=pl.ANY)
    smem = pl.BlockSpec(memory_space=pltpu.SMEM)
    wide = (1, rows, heads * HD)
    scratch = [
        pltpu.VMEM(wide, BF16),
        pltpu.VMEM(wide, BF16),
        pltpu.VMEM(wide, BF16),
        pltpu.VMEM((keys, cols), BF16),
        pltpu.VMEM((keys, cols), BF16),
        pltpu.VMEM((n, rows, dn), BF16),
        pltpu.VMEM((t, dt, cols), BF16),
        pltpu.VMEM((dn, keys), BF16),
        pltpu.VMEM((heads // 2, keys, 2 * rows), F32),
        pltpu.VMEM((groups, keys, HD), F32),
        pltpu.VMEM((groups, keys, HD), F32),
        pltpu.VMEM((keys, 2 * rows), F32),
        pltpu.VMEM((groups, n, rows, HD), BF16),
        pltpu.VMEM((groups, n - 1, rows, HD), BF16),
        pltpu.VMEM((groups, rows, HD), BF16),
        pltpu.VMEM((groups, n, rows, HD), BF16),
        pltpu.VMEM((groups, t, rows, HD), BF16),
        pltpu.VMEM((groups, n, rows, HD), BF16),
        pltpu.VMEM((groups, n - 1, rows, HD), BF16),
        pltpu.VMEM((groups, z * chunk, HD), BF16),
        pltpu.VMEM((groups, z - 1, chunk, HD), BF16),
        pltpu.VMEM((groups, chunk, HD), BF16),
        pltpu.VMEM((groups, z * chunk, HD), BF16),
        pltpu.SemaphoreType.DMA((5,)),
        pltpu.SemaphoreType.DMA((count,)),
        pltpu.SemaphoreType.DMA((count,)),
    ]
    return pl.pallas_call(
        functools.partial(kernel, sizes),
        out_shape=(
            jax.ShapeDtypeStruct(query_heads.shape, BF16),
            jax.ShapeDtypeStruct(key_heads.shape, BF16),
            jax.ShapeDtypeStruct(key_heads.shape, BF16),
            jax.ShapeDtypeStruct((1, rows, dt), BF16),
            jax.ShapeDtypeStruct((dn, cols), F32),
        ),
        in_specs=[smem, vmem, vmem, vmem] + [anywhere] * 5,
        out_specs=(vmem,) * 5,
        scratch_shapes=scratch,
        compiler_params=pltpu.CompilerParams(
            collective_id=0, has_side_effects=True, vmem_limit_bytes=56 * 1024 * 1024
        ),
    )(
        block_order, key_heads, value_heads, log_norm, hidden, query_heads, attention_out,
        output_grad, value_weight,
    )


def solution(mesh):
    placed = (
        P("dp", "ctx", None),
        P("dp", "ctx", "tp"),
        P("dp", "ctx", "tp"),
        P("dp", "ctx", "tp"),
        P("dp", "ctx", "tp"),
        P("dp", "ctx", "tp"),
        P("dp", "tp", "ctx"),
        P(),
        P(None, "tp"),
    )
    return jax.shard_map(
        shards,
        mesh=mesh,
        in_specs=placed,
        out_specs=(
            P("dp", "ctx", "tp"),
            P("dp", "ctx", "tp"),
            P("dp", "ctx", "tp"),
            P("dp", "ctx", "tp"),
            P("ctx", "tp"),
        ),
        check_vma=False,
    )
```

time: 175 us -> 64.7 us (0.37)
  waiting for transfers between devices: 113 us -> 0 us
  Pallas kernels: 0 us -> 55.9 us
  matrix products: 14.6 us -> 0 us
  between operations: 14 us -> 0.65 us
  blocking collectives: 13 us -> 0 us
  local copies, waits for them, and re-layouts: 15.3 us -> 7.77 us
  other arithmetic: 4.91 us -> 0 us
    reduce_scatter x4 -> x0, waiting for transfers between devices: 74.1 us -> none  [the longest x1 21.4 us: shards(): lax.psum_scatter(part_value.astype(jnp.bfloat16), 'ctx', scatter_dimensio...]
    pallas_call x0 -> x1, Pallas kernels: none -> 55.9 us  [shards(): pl.pallas_call(functools.partial(kernel, sizes), out_shape=(jax.ShapeDtyp...]
    psum x1 -> x0, waiting for transfers between devices: 38.4 us -> none  [shards(): summed_rows = lax.psum(row_share, 'dp').astype(jnp.float32)]
    dot_general x7 -> x0, matrix products: 14.6 us -> none  [the longest x1 3.58 us: attend(): jnp.einsum('tgjd,kgd->gjtk', grad_rows, value_block, preferred_element_ty...]
    all_gather x2 -> x0, blocking collectives: 13 us -> none  [the longest x1 7.25 us: shards(): lax.all_gather(key_local, 'ctx', axis=0, tiled=True)]
    unnamed x21 -> x7, local copies, waits for them, and re-layouts: 12.2 us -> 7.77 us
  transfers between devices with their start and end apart: 5 -> 0, of which waited for: 5 -> 0; matrix products, arithmetic and copies ran while one was open for 11% -> 0% of each run, Pallas kernels for 0% -> 0%
where the time goes in v1:
time: 64.7 us; the launch traced here: 64.4 us
  Pallas kernels  55.9 us (86%)
  local copies, waits for them, and re-layouts  7.77 us (12%)
  between operations  0.65 us (1%)
    pallas_call x1, Pallas kernels, shards(): pl.pallas_call(functools.partial(kernel, sizes), out_shape=(jax.ShapeDtyp...  55.9 us
    unnamed x7, local copies, waits for them, and re-layouts  7.77 us

profile of v1, /device:TPU:0, one launch (start us, length us, event | category | flops | bytes accessed | tf_op | source)
XLA Modules:
  0.0 64.4 jit_solution(18074518325401937916)
XLA Ops:
  0.6 55.9 %shard_map.128 = (bf16[1,128,2048]{2,1,0:T(8,128)(2,1)}, bf16[1,128,256]{2,1,0:T(8,128)(2,1)}, bf16[1,128,256]{2,1,0:T(8,128)(2,1)}, bf16[1,128,2048]{2,1,0:T(8,128)(2,1)}, f32[1024,256]{1,0:T(8,128)}) custom-call(s32[8]{0:T(128)} %order_ref.1, bf16[1,128,256]{2,1,0:T(8,128)(2,1)} %k_ref.1, bf16[1,128,256]{2,1,0:T(8,128)(2,1)} %v_ref.1, ...), custom_call_target="tpu_custom_call" | custom-call | tf_op jit(solution)/shard_map/pallas_call | solution.py:334
  56.6 0.0 copy-start
  56.6 2.0 %copy.19 = bf16[1,128,2048]{2,1,0:T(8,128)(2,1)} copy(bf16[1,128,2048]{2,1,0:T(8,128)(2,1)} %get-tuple-element.10) | data formatting | bytes 1048576
  58.6 1.5 %copy.20 = bf16[1,128,256]{2,1,0:T(8,128)(2,1)} copy(bf16[1,128,256]{2,1,0:T(8,128)(2,1)} %get-tuple-element.11) | data formatting | bytes 131072
  60.0 1.5 %copy.21 = bf16[1,128,256]{2,1,0:T(8,128)(2,1)} copy(bf16[1,128,256]{2,1,0:T(8,128)(2,1)} %get-tuple-element.12) | data formatting | bytes 131072
  61.5 1.9 %copy.22 = bf16[1,128,2048]{2,1,0:T(8,128)(2,1)} copy(bf16[1,128,2048]{2,1,0:T(8,128)(2,1)} %get-tuple-element.13) | data formatting | bytes 1048576
  63.4 0.0 copy-done
  63.4 1.0 %copy.23 = f32[1024,256]{1,0:T(8,128)} copy(f32[1024,256]{1,0:T(8,128)S(1)} %copy-done) | data formatting | bytes 2097152
Async XLA Ops:
  56.6 6.8 %copy-start = (f32[1024,256]{1,0:T(8,128)S(1)}, f32[1024,256]{1,0:T(8,128)}, u32[]{:S(2)}) copy-start(f32[1024,256]{1,0:T(8,128)} %get-tuple-element.14) | copy-start | bytes 3145732

commit v2 on v1

--- a/solution.py
+++ b/solution.py
@@ -13,6 +13,7 @@
 F32 = jnp.float32
 BF16 = jnp.bfloat16
 MESH = pl.DeviceIdType.MESH
+VMEM_LIMIT = 60 * 1024 * 1024
 
 
 def dot(a, b, ca, cb):
@@ -22,9 +23,9 @@
 def kernel(
     sizes,
     order_ref, k_ref, v_ref, norm_ref, hid_ref, q_ref, ao_ref, og_ref, vw_ref,
-    dq_ref, dk_ref, dv_ref, dh_ref, dw_ref,
+    dq_ref, dk_ref, dv_ref, dh_ref, zall,
     qs, aos, ogs, kg, vg, hg, wg, ht, prob, acck, accv, bias,
-    dvp, dvr, vown, vall, vtp, dkp, dkr, wp, zr, zown, zall,
+    dvp, dvr, vown, vall, vtp, dkp, dkr, wp, zr, zown,
     local_sem, send, recv,
 ):
     n, t, z, rows, groups, members, dn, dt, chunk, keyc = sizes
@@ -81,15 +82,23 @@
 
     my_rows = pl.ds(pl.multiple_of(me * rows, rows), rows)
     k_copies = fan("ctx", lambda p: k_ref.at[0], lambda o: kg.at[my_rows])
-    v_copies = fan("ctx", lambda p: v_ref.at[0], lambda o: vg.at[my_rows])
+    part = rows // t
+    my_part = pl.ds(pl.multiple_of(mt * part, 16), part)
     h_copies = fan(
         "ctx",
-        lambda p: hid_ref.at[0, :, pl.ds(pl.multiple_of(p * dn, 128), dn)],
-        lambda o: hg.at[me],
+        lambda p: hid_ref.at[0, my_part, pl.ds(pl.multiple_of(p * dn, 128), dn)],
+        lambda o: hg.at[me, my_part],
     )
-    w_copies = fan(
-        "tp", lambda p: vw_ref.at[pl.ds(pl.multiple_of(p * dt, 128), dt)], lambda o: wg.at[mt]
-    )
+    half = dt // 2
+
+    def weight_half(i):
+        return fan(
+            "tp",
+            lambda p: vw_ref.at[pl.ds(pl.multiple_of(p * dt + i * half, 128), half)],
+            lambda o: wg.at[mt, i * half : (i + 1) * half],
+        )
+
+    w_copies = weight_half(0)
     kg[my_rows] = k_ref[0]
     vg[my_rows] = v_ref[0]
 
@@ -222,25 +231,32 @@
         return made
 
     dv_copies = [values(g) for g in range(groups)]
+    v_copies = fan("ctx", lambda p: v_ref.at[0], lambda o: vg.at[my_rows])
+    loads[3].wait()
+    for copy in h_copies:
+        copy.wait_recv()
+    f_copies = []
+    for source in others("ctx"):
+        f_copies += fan(
+            "tp",
+            lambda p, source=source: hg.at[source, my_part],
+            lambda o, source=source: hg.at[source, my_part],
+        )
+    w_copies += weight_half(1)
     gathers, shares, dk_copies, w_parts = [], [], [], []
+    for g in range(groups):
+        made, made_tp = value_out(g, dv_copies[g])
+        gathers.append(made)
+        shares.append(made_tp)
     loads[2].wait()
     for copy in v_copies:
         copy.wait_recv()
-    made, made_tp = value_out(0, dv_copies[0])
-    gathers.append(made)
-    shares.append(made_tp)
     dk_copies.append(slopes(0))
-    for g in range(1, groups):
-        made, made_tp = value_out(g, dv_copies[g])
-        gathers.append(made)
-        shares.append(made_tp)
-    loads[3].wait()
-    for copy in h_copies:
+    for copy in f_copies:
         copy.wait_recv()
     for s in range(n):
         ht[:, s * rows : (s + 1) * rows] = hg[s].T
-    w_parts.append(weight_part(0, gathers[0]))
-    for g in range(1, groups):
+    for g in range(groups):
         w_parts.append(weight_part(g, gathers[g]))
     for g in range(1, groups):
         dk_copies.append(slopes(g))
@@ -270,17 +286,29 @@
         total = reduced(dk_copies[g], dkp[g, me].astype(F32), dkr, g)
         dk_ref[0, :, col : col + HD] = (total * scale).astype(BF16)
 
-    token_norm = (z * n * rows) ** (-0.5)
     for g in range(groups):
         for copy in z_copies[g]:
             copy.wait_recv()
-        dw_ref[:, g * HD : (g + 1) * HD] = zall[g, :dn].astype(F32) * token_norm
-
-    everything = k_copies + v_copies + h_copies + w_copies
+
+    everything = k_copies + v_copies + h_copies + w_copies + f_copies
     for group in dv_copies + gathers + shares + dk_copies + w_parts + z_copies:
         everything = everything + group
     for copy in everything:
         copy.wait_send()
+
+
+def finish(norm, *refs):
+    ins, outs, wide, sems = refs[:5], refs[5:10], refs[10], refs[11]
+    copies = [pltpu.make_async_copy(ins[i], outs[i], sems.at[i]) for i in range(4)]
+    for copy in copies:
+        copy.start()
+    total = ins[4]
+    for g in range(total.shape[0]):
+        wide[:, g * HD : (g + 1) * HD] = total[g, : wide.shape[0]].astype(F32) * norm
+    copies.append(pltpu.make_async_copy(wide, outs[4], sems.at[4]))
+    copies[4].start()
+    for copy in copies:
+        copy.wait()
 
 
 def shards(
@@ -299,7 +327,7 @@
     keys = n * rows
     keyc = min(keys, 512)
     sizes = (n, t, z, rows, groups, members, dn, dt, chunk, keyc)
-    count = (n - 1) * (3 + 3 * groups) + (t - 1) * (1 + groups) + (z - 1) * 2 * groups
+    count = (n - 1) * (3 + 3 * groups + t - 1) + (t - 1) * (2 + groups) + (z - 1) * 2 * groups
     vmem, anywhere = pl.BlockSpec(memory_space=pltpu.VMEM), pl.BlockSpec(memory_space=pl.ANY)
     smem = pl.BlockSpec(memory_space=pltpu.SMEM)
     wide = (1, rows, heads * HD)
@@ -326,13 +354,31 @@
         pltpu.VMEM((groups, z * chunk, HD), BF16),
         pltpu.VMEM((groups, z - 1, chunk, HD), BF16),
         pltpu.VMEM((groups, chunk, HD), BF16),
-        pltpu.VMEM((groups, z * chunk, HD), BF16),
         pltpu.SemaphoreType.DMA((5,)),
         pltpu.SemaphoreType.DMA((count,)),
         pltpu.SemaphoreType.DMA((count,)),
     ]
+    results = pl.pallas_call(
+        functools.partial(kernel, sizes),
+        out_shape=(
+            pltpu.VMEM(query_heads.shape, BF16),
+            pltpu.VMEM(key_heads.shape, BF16),
+            pltpu.VMEM(key_heads.shape, BF16),
+            pltpu.VMEM((1, rows, dt), BF16),
+            pltpu.VMEM((groups, z * chunk, HD), BF16),
+        ),
+        in_specs=[smem, vmem, vmem, vmem] + [anywhere] * 5,
+        out_specs=(vmem,) * 5,
+        scratch_shapes=scratch,
+        compiler_params=pltpu.CompilerParams(
+            collective_id=0, has_side_effects=True, vmem_limit_bytes=VMEM_LIMIT
+        ),
+    )(
+        block_order, key_heads, value_heads, log_norm, hidden, query_heads, attention_out,
+        output_grad, value_weight,
+    )
     return pl.pallas_call(
-        functools.partial(kernel, sizes),
+        functools.partial(finish, (z * n * rows) ** (-0.5)),
         out_shape=(
             jax.ShapeDtypeStruct(query_heads.shape, BF16),
             jax.ShapeDtypeStruct(key_heads.shape, BF16),
@@ -340,16 +386,10 @@
             jax.ShapeDtypeStruct((1, rows, dt), BF16),
             jax.ShapeDtypeStruct((dn, cols), F32),
         ),
-        in_specs=[smem, vmem, vmem, vmem] + [anywhere] * 5,
-        out_specs=(vmem,) * 5,
-        scratch_shapes=scratch,
-        compiler_params=pltpu.CompilerParams(
-            collective_id=0, has_side_effects=True, vmem_limit_bytes=56 * 1024 * 1024
-        ),
-    )(
-        block_order, key_heads, value_heads, log_norm, hidden, query_heads, attention_out,
-        output_grad, value_weight,
-    )
+        in_specs=[vmem] * 5,
+        out_specs=(anywhere,) * 5,
+        scratch_shapes=[pltpu.VMEM((dn, cols), F32), pltpu.SemaphoreType.DMA((5,))],
+    )(*results)
 
 
 def solution(mesh):

time: 64.7 us -> 60.9 us (0.941)
  local copies, waits for them, and re-layouts: 7.77 us -> 3.61 us
    unnamed x7 -> x10, local copies, waits for them, and re-layouts: 7.77 us -> 3.61 us
    pallas_call x1 -> x2, Pallas kernels: 55.9 us -> 56.4 us  [the longest x1 53.6 us: shards(): pl.pallas_call(functools.partial(kernel, sizes), out_shape=(pltpu.VMEM(qu...]
where the time goes in v2:
time: 60.9 us; the launch traced here: 60.7 us
  Pallas kernels  56.4 us (93%)
  local copies, waits for them, and re-layouts  3.61 us (6%)
  between operations  0.66 us (1%)
    pallas_call x1, Pallas kernels, shards(): pl.pallas_call(functools.partial(kernel, sizes), out_shape=(pltpu.VMEM(qu...  53.6 us
    unnamed x10, local copies, waits for them, and re-layouts  3.61 us
    pallas_call x1, Pallas kernels, shards(): pl.pallas_call(functools.partial(finish, (z * n * rows) ** (-0.5)), out_s...  2.81 us

profile of v2, /device:TPU:0, one launch (start us, length us, event | category | flops | bytes accessed | tf_op | source)
XLA Modules:
  0.0 60.7 jit_solution(9704850008801020785)
XLA Ops:
  0.6 53.6 %shard_map.128 = (bf16[1,128,2048]{2,1,0:T(8,128)(2,1)S(1)}, bf16[1,128,256]{2,1,0:T(8,128)(2,1)S(1)}, bf16[1,128,256]{2,1,0:T(8,128)(2,1)S(1)}, bf16[1,128,2048...) custom-call(s32[8]{0:T(128)} %order_ref.1, bf16[1,128,256]{2,1,0:T(8,128)(2,1)} %k_ref.1, bf16[1,128,256]{2,1,0:T(8,128)(2,1)} %v_ref.1, ...), custom_call_target="tpu_custom_call" | custom-call | tf_op jit(solution)/shard_map/pallas_call | solution.py:361
  54.2 0.0 copy-start
  54.2 0.8 %copy-done = bf16[1,128,2048]{2,1,0:T(8,128)(2,1)} copy-done((bf16[1,128,2048]{2,1,0:T(8,128)(2,1)}, bf16[1,128,2048]{2,1,0:T(8,128)(2,1)S(1)}, u32[]{:S(2)}) %copy-start) | copy-done | bytes 524312
  55.0 0.0 copy-start.1
  55.0 0.8 %copy-done.1 = bf16[1,128,2048]{2,1,0:T(8,128)(2,1)} copy-done((bf16[1,128,2048]{2,1,0:T(8,128)(2,1)}, bf16[1,128,2048]{2,1,0:T(8,128)(2,1)S(1)}, u32[]{:S(2)}) %copy-start.1) | copy-done | bytes 524312
  55.8 0.0 copy-start.2
  55.8 0.8 %copy-done.2 = bf16[2,1024,128]{2,1,0:T(8,128)(2,1)} copy-done((bf16[2,1024,128]{2,1,0:T(8,128)(2,1)}, bf16[2,1024,128]{2,1,0:T(8,128)(2,1)S(1)}, u32[]{:S(2)}) %copy-start.2) | copy-done | bytes 524312
  56.6 0.0 copy-start.3
  56.6 0.6 %copy-done.3 = bf16[1,128,256]{2,1,0:T(8,128)(2,1)} copy-done((bf16[1,128,256]{2,1,0:T(8,128)(2,1)}, bf16[1,128,256]{2,1,0:T(8,128)(2,1)S(1)}, u32[]{:S(2)}) %copy-start.3) | copy-done | bytes 65560
  57.2 0.0 copy-start.4
  57.2 0.6 %copy-done.4 = bf16[1,128,256]{2,1,0:T(8,128)(2,1)} copy-done((bf16[1,128,256]{2,1,0:T(8,128)(2,1)}, bf16[1,128,256]{2,1,0:T(8,128)(2,1)S(1)}, u32[]{:S(2)}) %copy-start.4) | copy-done | bytes 65560
  57.9 2.8 %shard_map.129 = (bf16[1,128,2048]{2,1,0:T(8,128)(2,1)}, bf16[1,128,256]{2,1,0:T(8,128)(2,1)}, bf16[1,128,256]{2,1,0:T(8,128)(2,1)}, bf16[1,128,2048]{2,1,0:T(8,128)(2,1)}, f32[1024,256]{1,0:T(8,128)}) custom-call(bf16[1,128,2048]{2,1,0:T(8,128)(2,1)} %copy-done, bf16[1,128,256]{2,1,0:T(8,128)(2,1)} %copy-done.3, bf16[1,128,256]{2,1,0:T(8,128)(2,1)} %copy-done.4, ...), custom_call_target="tpu_custom_call" | custom-call | tf_op jit(solution)/shard_map/pallas_call | solution.py:380
Async XLA Ops:
  54.2 0.8 %copy-start = (bf16[1,128,2048]{2,1,0:T(8,128)(2,1)}, bf16[1,128,2048]{2,1,0:T(8,128)(2,1)S(1)}, u32[]{:S(2)}) copy-start(bf16[1,128,2048]{2,1,0:T(8,128)(2,1)S(1)} %get-tuple-element.10.refs_0_) | copy-start | bytes 1572868
  55.0 0.8 %copy-start.1 = (bf16[1,128,2048]{2,1,0:T(8,128)(2,1)}, bf16[1,128,2048]{2,1,0:T(8,128)(2,1)S(1)}, u32[]{:S(2)}) copy-start(bf16[1,128,2048]{2,1,0:T(8,128)(2,1)S(1)} %get-tuple-element.13.refs_3_) | copy-start | bytes 1572868
  55.8 0.8 %copy-start.2 = (bf16[2,1024,128]{2,1,0:T(8,128)(2,1)}, bf16[2,1024,128]{2,1,0:T(8,128)(2,1)S(1)}, u32[]{:S(2)}) copy-start(bf16[2,1024,128]{2,1,0:T(8,128)(2,1)S(1)} %get-tuple-element.14.refs_4_) | copy-start | bytes 1572868
  56.6 0.6 %copy-start.3 = (bf16[1,128,256]{2,1,0:T(8,128)(2,1)}, bf16[1,128,256]{2,1,0:T(8,128)(2,1)S(1)}, u32[]{:S(2)}) copy-start(bf16[1,128,256]{2,1,0:T(8,128)(2,1)S(1)} %get-tuple-element.11.refs_1_) | copy-start | bytes 196612
  57.2 0.6 %copy-start.4 = (bf16[1,128,256]{2,1,0:T(8,128)(2,1)}, bf16[1,128,256]{2,1,0:T(8,128)(2,1)S(1)}, u32[]{:S(2)}) copy-start(bf16[1,128,256]{2,1,0:T(8,128)(2,1)S(1)} %get-tuple-element.12.refs_2_) | copy-start | bytes 196612

commit v3 on v2

--- a/solution.py
+++ b/solution.py
@@ -25,8 +25,8 @@
     order_ref, k_ref, v_ref, norm_ref, hid_ref, q_ref, ao_ref, og_ref, vw_ref,
     dq_ref, dk_ref, dv_ref, dh_ref, zall,
     qs, aos, ogs, kg, vg, hg, wg, ht, prob, acck, accv, bias,
-    dvp, dvr, vown, vall, vtp, dkp, dkr, wp, zr, zown,
-    local_sem, send, recv,
+    dvp, dvr, vown, vall, vtp, dkp, dkr, wp, zr, zs, zacc,
+    local_sem, send, recv, zsend, zrecv,
 ):
     n, t, z, rows, groups, members, dn, dt, chunk, keyc = sizes
     me, mt, mz = lax.axis_index("ctx"), lax.axis_index("tp"), lax.axis_index("dp")
@@ -84,21 +84,36 @@
     k_copies = fan("ctx", lambda p: k_ref.at[0], lambda o: kg.at[my_rows])
     part = rows // t
     my_part = pl.ds(pl.multiple_of(mt * part, 16), part)
-    h_copies = fan(
-        "ctx",
-        lambda p: hid_ref.at[0, my_part, pl.ds(pl.multiple_of(p * dn, 128), dn)],
-        lambda o: hg.at[me, my_part],
-    )
     half = dt // 2
-
-    def weight_half(i):
-        return fan(
-            "tp",
-            lambda p: vw_ref.at[pl.ds(pl.multiple_of(p * dt + i * half, 128), half)],
-            lambda o: wg.at[mt, i * half : (i + 1) * half],
+    parity = me % 2
+    hops = n // 2
+    near = me + 1 - 2 * parity
+    fars = [(k, c) for k in range(1, hops) for c in range(2)]
+
+    def far(k, c):
+        return lax.rem(me // 2 + k + hops, hops) * 2 + lax.rem(parity + c + 2, 2)
+
+    def one(axis, peer, source, target):
+        copy = pltpu.make_async_remote_copy(
+            src_ref=source,
+            dst_ref=target,
+            send_sem=send.at[used[0]],
+            recv_sem=recv.at[used[0]],
+            device_id={axis: peer},
+            device_id_type=MESH,
         )
-
-    w_copies = weight_half(0)
+        used[0] += 1
+        copy.start()
+        return copy
+
+    def columns(p):
+        return pl.ds(pl.multiple_of(p * dn, 128), dn)
+
+    h_copies = [
+        one("ctx", far(k, c), hid_ref.at[0, my_part, columns(far(k, c))], hg.at[me, my_part])
+        for k, c in fars
+    ]
+    near_copy = one("ctx", near, hid_ref.at[0, :, columns(near)], hg.at[me])
     kg[my_rows] = k_ref[0]
     vg[my_rows] = v_ref[0]
 
@@ -212,58 +227,154 @@
         if z * chunk > dn:
             wp[g, dn:] = jnp.zeros((z * chunk - dn, HD), BF16)
 
-        def piece(p):
-            return wp.at[g, pl.ds(pl.multiple_of(p * chunk, 16), chunk)]
-
-        return fan("dp", piece, lambda o: zr.at[g, o])
-
-    def weight_sum(g, copies):
-        for copy in copies:
-            copy.wait_recv()
-        mine = pl.ds(pl.multiple_of(mz * chunk, 16), chunk)
-        total = wp[g, mine].astype(F32)
-        for o in range(z - 1):
-            total = total + zr[g, o].astype(F32)
-        total = total.astype(BF16)
-        zown[g] = total
-        made = fan("dp", lambda p: zown.at[g], lambda o: zall.at[g, mine])
-        zall[g, mine] = total
-        return made
+    def hop(source, target, phase, flow, g, index):
+        to = lax.rem(mz + 1, z) if flow == 0 else lax.rem(mz + z - 1, z)
+        return pltpu.make_async_remote_copy(
+            src_ref=source,
+            dst_ref=target,
+            send_sem=zsend.at[phase, flow, g, index],
+            recv_sem=zrecv.at[phase, flow, g, index],
+            device_id={"dp": to},
+            device_id_type=MESH,
+        )
+
+    def sender(flow, owner):
+        return mz < owner if flow == 0 else mz > owner
+
+    def inner(flow):
+        return mz > 0 if flow == 0 else mz < z - 1
+
+    def outer(flow):
+        return mz < z - 1 if flow == 0 else mz > 0
+
+    def sum_hop(flow, g, owner):
+        return hop(zs.at[flow, g, owner], zr.at[flow, g, owner], 0, flow, g, owner)
+
+    def line_step(flow, g, owner):
+        mine = slice(owner * chunk, (owner + 1) * chunk)
+
+        @pl.when(sender(flow, owner))
+        def _():
+            zs[flow, g, owner] = wp[g, mine]
+
+            @pl.when(inner(flow))
+            def _():
+                sum_hop(flow, g, owner).wait_recv()
+                total = wp[g, mine].astype(F32) + zr[flow, g, owner].astype(F32)
+                zs[flow, g, owner] = total.astype(BF16)
+
+            sum_hop(flow, g, owner).start()
+
+    def block_of(index):
+        return pl.ds(pl.multiple_of(index * chunk, 16), chunk)
+
+    def spread_hop(flow, g, index):
+        at = block_of(index)
+        return hop(zall.at[g, at], zall.at[g, at], 1, flow, g, index)
+
+    def line_own(g):
+        zacc[...] = wp[g, block_of(mz)].astype(F32)
+        for flow in range(2):
+
+            @pl.when(inner(flow))
+            def _():
+                sum_hop(flow, g, mz).wait_recv()
+                zacc[...] += zr[flow, g, mz].astype(F32)
+
+        zall[g, block_of(mz)] = zacc[...].astype(BF16)
+        for flow in range(2):
+
+            @pl.when(outer(flow))
+            def _():
+                spread_hop(flow, g, mz).start()
+
+    def line_pass(flow, g, d):
+        there = mz >= d if flow == 0 else mz + d < z
+
+        @pl.when(there)
+        def _():
+            index = mz - d if flow == 0 else mz + d
+            spread_hop(flow, g, index).wait_recv()
+
+            @pl.when(outer(flow))
+            def _():
+                spread_hop(flow, g, index).start()
+
+    def line_drain():
+        for flow in range(2):
+            for g in range(groups):
+                for owner in range(z):
+
+                    @pl.when(sender(flow, owner))
+                    def _():
+                        sum_hop(flow, g, owner).wait_send()
+
+                    passed = mz >= owner if flow == 0 else mz <= owner
+
+                    @pl.when(jnp.logical_and(passed, outer(flow)))
+                    def _():
+                        spread_hop(flow, g, owner).wait_send()
 
     dv_copies = [values(g) for g in range(groups)]
-    v_copies = fan("ctx", lambda p: v_ref.at[0], lambda o: vg.at[my_rows])
-    loads[3].wait()
-    for copy in h_copies:
+    f_copies = []
+    for (k, c), copy in zip(fars, h_copies):
         copy.wait_recv()
-    f_copies = []
-    for source in others("ctx"):
+        source = far(-k, -c)
         f_copies += fan(
             "tp",
-            lambda p, source=source: hg.at[source, my_part],
-            lambda o, source=source: hg.at[source, my_part],
+            lambda p: hg.at[source, my_part],
+            lambda o: hg.at[source, my_part],
         )
-    w_copies += weight_half(1)
-    gathers, shares, dk_copies, w_parts = [], [], [], []
+    my_half = pl.ds(pl.multiple_of(parity * half, 16), half)
+    w_copies = fan(
+        "tp",
+        lambda p: vw_ref.at[pl.ds(pl.multiple_of(p * dt + parity * half, 16), half)],
+        lambda o: wg.at[mt, my_half],
+    )
+    gathers, shares = [], []
     for g in range(groups):
         made, made_tp = value_out(g, dv_copies[g])
         gathers.append(made)
         shares.append(made_tp)
-    loads[2].wait()
-    for copy in v_copies:
-        copy.wait_recv()
-    dk_copies.append(slopes(0))
+    v_copies = fan("ctx", lambda p: v_ref.at[0], lambda o: vg.at[my_rows])
+    loads[3].wait()
+    near_copy.wait_recv()
     for copy in f_copies:
         copy.wait_recv()
     for s in range(n):
         ht[:, s * rows : (s + 1) * rows] = hg[s].T
     for g in range(groups):
-        w_parts.append(weight_part(g, gathers[g]))
+        weight_part(g, gathers[g])
+
+    def line_round(j):
+        for g in range(groups):
+            line_step(0, g, z - 1 - j)
+            line_step(1, g, j)
+
+    loads[2].wait()
+    for copy in v_copies:
+        copy.wait_recv()
+    line_round(0)
+    dk_copies = [slopes(0)]
+    for j in range(1, z - 1):
+        line_round(j)
     for g in range(1, groups):
         dk_copies.append(slopes(g))
-    z_copies = [weight_sum(g, w_parts[g]) for g in range(groups)]
+    for g in range(groups):
+        line_own(g)
+    for copy in w_copies:
+        copy.wait_recv()
+    relays = []
+    for o in range(1, t):
+        source = lax.rem(mt + t - o, t)
+        relays.append(one("ctx", near, wg.at[source, my_half], wg.at[source, my_half]))
+    for d in range(1, z):
+        for g in range(groups):
+            for flow in range(2):
+                line_pass(flow, g, d)
 
     loads[4].wait()
-    for copy in w_copies:
+    for copy in relays:
         copy.wait_recv()
     for g in range(groups):
         for copy in shares[g]:
@@ -286,12 +397,9 @@
         total = reduced(dk_copies[g], dkp[g, me].astype(F32), dkr, g)
         dk_ref[0, :, col : col + HD] = (total * scale).astype(BF16)
 
-    for g in range(groups):
-        for copy in z_copies[g]:
-            copy.wait_recv()
-
-    everything = k_copies + v_copies + h_copies + w_copies + f_copies
-    for group in dv_copies + gathers + shares + dk_copies + w_parts + z_copies:
+    line_drain()
+    everything = k_copies + v_copies + h_copies + w_copies + f_copies + relays + [near_copy]
+    for group in dv_copies + gathers + shares + dk_copies:
         everything = everything + group
     for copy in everything:
         copy.wait_send()
@@ -327,8 +435,8 @@
     keys = n * rows
     keyc = min(keys, 512)
     sizes = (n, t, z, rows, groups, members, dn, dt, chunk, keyc)
-    count = (n - 1) * (3 + 3 * groups + t - 1) + (t - 1) * (2 + groups) + (z - 1) * 2 * groups
-    vmem, anywhere = pl.BlockSpec(memory_space=pltpu.VMEM), pl.BlockSpec(memory_space=pl.ANY)
+    count = (n - 1) * (3 + 3 * groups + t - 1) + (t - 1) * (2 + groups)
+    vmem, anywhere = pl.BlockSpec(memory_space=pltpu.VMEM), pl.BlockSpec(memory_space=pltpu.HBM)
     smem = pl.BlockSpec(memory_space=pltpu.SMEM)
     wide = (1, rows, heads * HD)
     scratch = [
@@ -352,11 +460,14 @@
         pltpu.VMEM((groups, n, rows, HD), BF16),
         pltpu.VMEM((groups, n - 1, rows, HD), BF16),
         pltpu.VMEM((groups, z * chunk, HD), BF16),
-        pltpu.VMEM((groups, z - 1, chunk, HD), BF16),
-        pltpu.VMEM((groups, chunk, HD), BF16),
+        pltpu.VMEM((2, groups, z, chunk, HD), BF16),
+        pltpu.VMEM((2, groups, z, chunk, HD), BF16),
+        pltpu.VMEM((chunk, HD), F32),
         pltpu.SemaphoreType.DMA((5,)),
         pltpu.SemaphoreType.DMA((count,)),
         pltpu.SemaphoreType.DMA((count,)),
+        pltpu.SemaphoreType.DMA((2, 2, groups, z)),
+        pltpu.SemaphoreType.DMA((2, 2, groups, z)),
     ]
     results = pl.pallas_call(
         functools.partial(kernel, sizes),
@@ -389,6 +500,7 @@
         in_specs=[vmem] * 5,
         out_specs=(anywhere,) * 5,
         scratch_shapes=[pltpu.VMEM((dn, cols), F32), pltpu.SemaphoreType.DMA((5,))],
+        compiler_params=pltpu.CompilerParams(vmem_limit_bytes=16 * 1024 * 1024),
     )(*results)
 
 

time: 60.9 us -> 62.7 us (1.030)
  Pallas kernels: 56.4 us -> 61.9 us
  local copies, waits for them, and re-layouts: 3.61 us -> 0 us
    pallas_call x1, Pallas kernels: 53.6 us -> 60.5 us  [shards(): pl.pallas_call(functools.partial(kernel, sizes), out_shape=(pltpu.VMEM(qu...]
    unnamed x10 -> x0, local copies, waits for them, and re-layouts: 3.61 us -> none
    pallas_call x1, Pallas kernels: 2.81 us -> 1.4 us  [shards(): pl.pallas_call(functools.partial(finish, (z * n * rows) ** (-0.5)), out_s...]
where the time goes in v3:
time: 62.7 us; the launch traced here: 62.6 us
  Pallas kernels  61.9 us (99%)
  between operations  0.64 us (1%)
    pallas_call x1, Pallas kernels, shards(): pl.pallas_call(functools.partial(kernel, sizes), out_shape=(pltpu.VMEM(qu...  60.5 us
    pallas_call x1, Pallas kernels, shards(): pl.pallas_call(functools.partial(finish, (z * n * rows) ** (-0.5)), out_s...  1.4 us

profile of v3, /device:TPU:0, one launch (start us, length us, event | category | flops | bytes accessed | tf_op | source)
XLA Modules:
  0.0 62.6 jit_solution(3779714429057984421)
XLA Ops:
  0.6 60.5 %shard_map.128 = (bf16[1,128,2048]{2,1,0:T(8,128)(2,1)S(1)}, bf16[1,128,256]{2,1,0:T(8,128)(2,1)S(1)}, bf16[1,128,256]{2,1,0:T(8,128)(2,1)S(1)}, bf16[1,128,2048...) custom-call(s32[8]{0:T(128)} %order_ref.1, bf16[1,128,256]{2,1,0:T(8,128)(2,1)} %k_ref.1, bf16[1,128,256]{2,1,0:T(8,128)(2,1)} %v_ref.1, ...), custom_call_target="tpu_custom_call" | custom-call | tf_op jit(solution)/shard_map/pallas_call | solution.py:472
  61.2 1.4 %shard_map.129 = (bf16[1,128,2048]{2,1,0:T(8,128)(2,1)}, bf16[1,128,256]{2,1,0:T(8,128)(2,1)}, bf16[1,128,256]{2,1,0:T(8,128)(2,1)}, bf16[1,128,2048]{2,1,0:T(8,128)(2,1)}, f32[1024,256]{1,0:T(8,128)}) custom-call(bf16[1,128,2048]{2,1,0:T(8,128)(2,1)S(1)} %get-tuple-element.10.refs_0_, bf16[1,128,256]{2,1,0:T(8,128)(2,1)S(1)} %get-tuple-element.11.refs_1_, ...), custom_call_target="tpu_custom_call" | custom-call | tf_op jit(solution)/shard_map/pallas_call | solution.py:491
